TPU v7x, 32 devices: a whole 2x2x4 slice. The times are simulated.
32 devices in a mesh: pix: 32 (over z, y, x, core).
Axes of the slice: x: 2, y: 2, z: 4, core: 2. Of those that a mesh axis runs over, the one named last changes fastest.
Arguments:
- green: float32 [2048, 6144], P('pix'), may hold values from -200 to 200, as said below
- sketch: float32 [6144, 128], P('pix'), may hold values from -0.078125 to 0.078125
Outputs:
- basis: float32 [2048, 128], P('pix')
- projection: float32 [6144, 128], P('pix')
- spectrum_gram: float32 [128, 128], replicated
Inputs may be any that keep to these rules, and one draw needn't show every extreme that they name: `green`: finite real entries; each patch's column has its own scale.
All inputs are finite; a program needn't handle non-finite values.
Results may differ from a plain program's by a relative error of at most 0.000086.
Values sent between devices are 32-bit elements; how exact they have to be, the bound alone decides.
No kernel may reach another device: no remote copies, remote signals or barrier semaphores. Data moves between devices by JAX's collectives and lax.ppermute only.
A program may use at most 64 MiB of HBM per device.

v0:
```python
import jax
import jax.numpy as jnp
from jax import lax
from jax.sharding import PartitionSpec as P

PATCHES = 6144


def body(green, sketch):
    highest = lax.Precision.HIGHEST
    rows_here = green.shape[0]
    devices_pix = lax.axis_size("pix")
    total_pixels = rows_here * devices_pix
    columns = green
    sketched = jnp.dot(
        columns,
        lax.all_gather(sketch, "pix", axis=0, tiled=True),
        precision=highest,
        preferred_element_type=jnp.float32,
    )
    local_gram = jnp.dot(
        sketched.T, sketched, precision=highest, preferred_element_type=jnp.float32
    )
    columns = green
    raw_proj = lax.psum_scatter(
        lax.dot_general(
            columns,
            sketched,
            (((0,), (0,)), ((), ())),
            precision=highest,
            preferred_element_type=jnp.float32,
        ),
        "pix",
        scatter_dimension=0,
        tiled=True,
    )
    gram = lax.psum(local_gram, "pix")
    lower = jnp.linalg.cholesky(gram)
    orthonormal = jax.scipy.linalg.solve_triangular(lower, sketched.T, lower=True).T
    projection = jax.scipy.linalg.solve_triangular(lower, raw_proj.T, lower=True).T
    basis = jnp.sqrt(jnp.float32(total_pixels)) * orthonormal
    local_spec = jnp.dot(
        projection.T, projection, precision=highest, preferred_element_type=jnp.float32
    )
    spectrum_gram = lax.psum(local_spec, "pix") / jnp.float32(PATCHES)
    return (basis, projection, spectrum_gram)


def solution(mesh):
    in_specs = (P("pix", None), P("pix", None))
    out_specs = (P("pix", None), P("pix", None), P())
    return jax.shard_map(body, mesh=mesh, in_specs=in_specs, out_specs=out_specs, check_vma=False)
```

profile of v0, /device:TPU:1, one launch (start us, length us, event | category | flops | bytes accessed | tf_op | source)
XLA Modules:
  0.0 439.5 jit_solution(5103394524616839399)
XLA Ops:
  7.2 0.0 all-gather.2.cloned.1.call-start
  7.2 0.7 all-gather.2.cloned.1.call-update
  7.9 0.0 all-reduce.3.cloned.1.call-start
  8.0 64.5 %all-gather.2.cloned.1.call-done = f32[6144,128]{1,0:T(8,128)} async-done(((f32[192,128]{1,0:T(8,128)}), f32[6144,128]{1,0:T(8,128)}) %all-gather.2.cloned.1.call-update) | async-done | bytes 3145744 | tf_op jit(solution)/shard_map/all_gather | solution.py:17
  72.4 3.9 fusion.5
  76.3 0.9 fusion.6
  77.3 0.0 reduce-scatter.4.cloned.1.call-start
  77.3 4.4 convolution_bitcast_fusion
  81.7 3.6 copy.10
  85.2 0.0 reduce-scatter.4.cloned.1.call-update
  85.3 0.2 all-reduce.5.cloned.1.call-start
  85.5 112.7 %all-reduce.3.cloned.1.call-done = f32[128,128]{0,1:T(8,128)} async-done(((f32[128,128]{0,1:T(8,128)}), f32[128,128]{0,1:T(8,128)}) %all-reduce.3.cloned.1.call-update) | async-done | bytes 65552 | tf_op jit(solution)/shard_map/psum | solution.py:37
  198.2 0.9 copy.8
  199.1 0.9 fusion.4
  200.0 11.7 %cholesky.16 = f32[128,128]{1,0:T(8,128)S(1)} custom-call(f32[128,128]{1,0:T(8,128)S(1)} %fusion.4), custom_call_target="Cholesky" | custom-call | tf_op jit(solution)/shard_map/jit(cholesky)/cholesky | solution.py:38
  211.7 0.6 compare_reduce_fusion
  212.4 0.7 fusion
  213.0 9.8 %custom-call.10 = f32[1,128,128]{1,2,0:T(8,128)S(1)} custom-call(f32[1,128,128]{2,1,0:T(8,128)S(1)} %fusion), custom_call_target="InvertDiagBlocksLowerTriangular" | custom-call | tf_op jit(solution)/shard_map/jit(_solve_triangular)/triangular_solve | solution.py:39
  222.9 80.8 %reduce-scatter.4.cloned.1.call-done = f32[192,128]{1,0:T(8,128)} async-done(((f32[6144,128]{1,0:T(8,128)}), f32[192,128]{1,0:T(8,128)}) %reduce-scatter.4.cloned.1.call-update) | async-done | bytes 98320
  303.6 1.1 fusion.1
  304.8 1.1 fusion.7
  305.9 0.8 convolution_multiply_fusion
  306.7 124.8 %all-reduce.5.cloned.1.call-done = f32[128,128]{1,0:T(8,128)} async-done(((f32[128,128]{1,0:T(8,128)}), f32[128,128]{1,0:T(8,128)}) %all-reduce.5.cloned.1.call-update) | async-done | bytes 65552 | tf_op jit(solution)/shard_map/psum | solution.py:45
  431.5 1.5 broadcast_multiply_fusion
  (7 shorter events, 0.1 us)
Async XLA Ops:
  7.2 65.3 %copy-start = (f32[64,6144]{1,0:T(8,128)S(1)}, f32[64,6144]{1,0:T(8,128)}, u32[]{:S(2)}) copy-start(f32[64,6144]{1,0:T(8,128)} %param.2) | copy-start | bytes 4718596
  7.2 65.2 %all-gather.2.cloned.1.call-start = ((), (), s32[]{:S(2)}) async-start(), calls=%async_computation.1 | async-start | bytes 3244032 | tf_op jit(solution)/shard_map/all_gather | solution.py:17
  7.9 190.3 %all-reduce.3.cloned.1.call-start = ((), (), s32[]{:S(2)}) async-start(), calls=%async_computation.2 | async-start | bytes 131072 | tf_op jit(solution)/shard_map/psum | solution.py:37
  77.3 226.4 %reduce-scatter.4.cloned.1.call-start = ((), (), s32[]{:S(2)}) async-start(), calls=%async_computation.4 | async-start | bytes 3244032
  85.3 346.3 %all-reduce.5.cloned.1.call-start = ((), (), s32[]{:S(2)}) async-start(), calls=%async_computation.3 | async-start | bytes 131072 | tf_op jit(solution)/shard_map/psum | solution.py:45
  304.8 128.2 %copy-start.1 = (f32[128,192]{0,1:T(8,128)}, f32[128,192]{0,1:T(8,128)S(1)}, u32[]{:S(2)}) copy-start(f32[128,192]{0,1:T(8,128)S(1)} %fusion.1) | copy-start | bytes 294916
Sparse Core Ops, SparseCore 0:
  10.9 61.5 all-gather.1
  78.6 119.5 all-reduce.2
  203.6 99.9 reduce-scatter.3
  309.6 121.8 all-reduce.4
where the time goes:
time: 440 us
  waiting for transfers between devices  384 us (87%)
  other arithmetic  25.2 us (6%)
  between operations  13.8 us (3%)
  matrix products  12.2 us (3%)
  local copies, waits for them, and re-layouts  4.5 us (1%)
    psum x1, waiting for transfers between devices, body(): spectrum_gram = lax.psum(local_spec, 'pix') / jnp.float32(PATCHES)  125 us
    psum x1, waiting for transfers between devices, body(): gram = lax.psum(local_gram, 'pix')  113 us
    unnamed x5, waiting for transfers between devices  81.5 us
    all_gather x1, waiting for transfers between devices, body(): lax.all_gather(sketch, 'pix', axis=0, tiled=True)  64.5 us
    another operation x3, other arithmetic, body(): lower = jnp.linalg.cholesky(gram)  12.4 us
    another operation x2, other arithmetic, body(): jax.scipy.linalg.solve_triangular(lower, sketched.T, lower=True)  10.5 us
  transfers between devices with their start and end apart: 4, of which 4 were waited for; matrix products, arithmetic and copies ran while one was open for 8% of the time, Pallas kernels for 0%

commit v1 on v0

--- a/solution.py
+++ b/solution.py
@@ -34,7 +34,8 @@
         scatter_dimension=0,
         tiled=True,
     )
-    gram = lax.psum(local_gram, "pix")
+    point_task = lambda z: lax.all_gather(z, "pix").sum(axis=0)
+    gram = point_task(local_gram)
     lower = jnp.linalg.cholesky(gram)
     orthonormal = jax.scipy.linalg.solve_triangular(lower, sketched.T, lower=True).T
     projection = jax.scipy.linalg.solve_triangular(lower, raw_proj.T, lower=True).T

time: 440 us -> 373 us (0.85)
  waiting for transfers between devices: 384 us -> 317 us
    psum x1 -> x0, waiting for transfers between devices: 113 us -> none  [body(): gram = lax.psum(local_gram, 'pix')]
    all_gather x0 -> x1, waiting for transfers between devices: none -> 46.8 us  [body(): point_task = lambda z: lax.all_gather(z, 'pix').sum(axis=0)]
  transfers between devices with their start and end apart: 4 -> 4, of which waited for: 4 -> 4; matrix products, arithmetic and copies ran while one was open for 8% -> 9% of each run, Pallas kernels for 0% -> 0%
where the time goes in v1:
time: 373 us
  waiting for transfers between devices  317 us (85%)
  other arithmetic  26 us (7%)
  between operations  13.8 us (4%)
  matrix products  12.2 us (3%)
    psum x1, waiting for transfers between devices, body(): spectrum_gram = lax.psum(local_spec, 'pix') / jnp.float32(PATCHES)  125 us
    unnamed x5, waiting for transfers between devices  80.6 us
    all_gather x1, waiting for transfers between devices, body(): lax.all_gather(sketch, 'pix', axis=0, tiled=True)  64.5 us
    all_gather x1, waiting for transfers between devices, body(): point_task = lambda z: lax.all_gather(z, 'pix').sum(axis=0)  46.8 us
    another operation x3, other arithmetic, body(): lower = jnp.linalg.cholesky(gram)  12.4 us
    another operation x2, other arithmetic, body(): jax.scipy.linalg.solve_triangular(lower, sketched.T, lower=True)  10.5 us
  transfers between devices with their start and end apart: 4, of which 4 were waited for; matrix products, arithmetic and copies ran while one was open for 9% of the time, Pallas kernels for 0%

profile of v1, /device:TPU:1, one launch (start us, length us, event | category | flops | bytes accessed | tf_op | source)
XLA Modules:
  0.0 372.9 jit_solution(11978824645821925223)
XLA Ops:
  7.2 0.0 all-gather.4.cloned.1.call-start
  7.2 0.7 all-gather.4.cloned.1.call-update
  7.9 0.0 all-gather.6.cloned.1.call-start
  8.0 64.5 %all-gather.4.cloned.1.call-done = f32[6144,128]{1,0:T(8,128)} async-done(((f32[192,128]{1,0:T(8,128)}), f32[6144,128]{1,0:T(8,128)}) %all-gather.4.cloned.1.call-update) | async-done | bytes 3145744 | tf_op jit(solution)/shard_map/all_gather | solution.py:17
  72.4 3.9 %fusion.5 = f32[64,128]{1,0:T(8,128)S(1)} fusion(f32[64,6144]{1,0:T(8,128)S(1)} %copy-done, f32[6144,128]{1,0:T(8,128)} %all-gather.4.cloned.1.call-done), kind=kOutput, calls=%fused_computation.14 | convolution fusion | flops 603979776 | bytes 4751360 | tf_op jit(solution)/shard_map/dot_general | solution.py:15
  76.3 0.9 fusion.6
  77.3 0.0 all-gather.6.cloned.1.call-update
  77.3 0.0 reduce-scatter.4.cloned.1.call-start
  77.3 4.4 %convolution_bitcast_fusion = f32[6144,128]{0,1:T(8,128)} fusion(f32[64,128]{1,0:T(8,128)S(1)} %fusion.5, f32[64,6144]{1,0:T(8,128)S(1)} %copy-done), kind=kOutput, calls=%fused_computation | convolution fusion | flops 603979776 | bytes 4751360 | tf_op jit(solution)/shard_map/dot_general | solution.py:26
  81.7 3.5 copy.7
  85.3 0.2 all-reduce.2.cloned.1.call-start
  85.5 46.8 %all-gather.6.cloned.1.call-done = f32[4096,128]{1,0:T(8,128)} async-done(((f32[128,128]{1,0:T(8,128)}), f32[4096,128]{1,0:T(8,128)}) %all-gather.6.cloned.1.call-update) | async-done | bytes 2097168 | tf_op jit(solution)/shard_map/all_gather | solution.py:37
  132.3 1.7 reduce_sum.9
  134.0 0.1 copy.6
  134.2 11.7 %cholesky.16 = f32[128,128]{1,0:T(8,128)S(1)} custom-call(f32[128,128]{1,0:T(8,128)S(1)} %fusion.4), custom_call_target="Cholesky" | custom-call | tf_op jit(solution)/shard_map/jit(cholesky)/cholesky | solution.py:39
  145.9 0.6 compare_reduce_fusion
  146.5 0.7 fusion
  147.2 9.8 %custom-call.10 = f32[1,128,128]{1,2,0:T(8,128)S(1)} custom-call(f32[1,128,128]{2,1,0:T(8,128)S(1)} %fusion), custom_call_target="InvertDiagBlocksLowerTriangular" | custom-call | tf_op jit(solution)/shard_map/jit(_solve_triangular)/triangular_solve | solution.py:40
  157.0 79.9 %reduce-scatter.4.cloned.1.call-done = f32[192,128]{1,0:T(8,128)} async-done(((f32[6144,128]{1,0:T(8,128)}), f32[192,128]{1,0:T(8,128)}) %reduce-scatter.4.cloned.1.call-update) | async-done | bytes 98320
  236.9 1.1 fusion.1
  238.1 1.1 fusion.7
  239.2 0.8 convolution_multiply_fusion
  240.0 125.0 %all-reduce.2.cloned.1.call-done = f32[128,128]{1,0:T(8,128)} async-done(((f32[128,128]{1,0:T(8,128)}), f32[128,128]{1,0:T(8,128)}) %all-reduce.2.cloned.1.call-update) | async-done | bytes 65552 | tf_op jit(solution)/shard_map/psum | solution.py:46
  364.9 1.5 broadcast_multiply_fusion
  (8 shorter events, 0.1 us)
Async XLA Ops:
  7.2 65.3 %copy-start = (f32[64,6144]{1,0:T(8,128)S(1)}, f32[64,6144]{1,0:T(8,128)}, u32[]{:S(2)}) copy-start(f32[64,6144]{1,0:T(8,128)} %param.2) | copy-start | bytes 4718596
  7.2 65.2 %all-gather.4.cloned.1.call-start = ((), (), s32[]{:S(2)}) async-start(), calls=%async_computation.1 | async-start | bytes 3244032 | tf_op jit(solution)/shard_map/all_gather | solution.py:17
  7.9 124.4 %all-gather.6.cloned.1.call-start = ((), (), s32[]{:S(2)}) async-start(), calls=%async_computation.3 | async-start | bytes 2162688 | tf_op jit(solution)/shard_map/all_gather | solution.py:37
  77.3 159.6 %reduce-scatter.4.cloned.1.call-start = ((), (), s32[]{:S(2)}) async-start(), calls=%async_computation.4 | async-start | bytes 3244032
  85.3 279.7 %all-reduce.2.cloned.1.call-start = ((), (), s32[]{:S(2)}) async-start(), calls=%async_computation.2 | async-start | bytes 131072 | tf_op jit(solution)/shard_map/psum | solution.py:46
  238.1 128.4 %copy-start.1 = (f32[128,192]{0,1:T(8,128)}, f32[128,192]{0,1:T(8,128)S(1)}, u32[]{:S(2)}) copy-start(f32[128,192]{0,1:T(8,128)S(1)} %fusion.1) | copy-start | bytes 294916
Sparse Core Ops, SparseCore 0:
  10.9 61.5 all-gather.3
  77.4 54.8 all-gather.5
  137.8 99.0 reduce-scatter.3
  242.9 121.9 all-reduce.1
